TPU v7x, 32 devices: a whole 2x2x4 slice. The times are simulated.
32 devices in a mesh: dp: 8 (over y, x, core), mp: 4 (over z).
Axes of the slice: x: 2, y: 2, z: 4, core: 2. Of those that a mesh axis runs over, the one named last changes fastest.
Arguments:
- slab_values: bfloat16 [32, 32, 2048], P(('dp', 'mp')), may hold values from -6 to 6
- row_ids: int32 [32, 32, 32], P(('dp', 'mp')), may hold values from 0 to 4095, as said below
- peer_counts: int32 [32, 32], P(('dp', 'mp')), may hold values from 1 to 32, as said below
- lookup_slots: int32 [8192, 16], P(('dp', 'mp')), may hold values from 0 to 1023, as said below
- labels: int32 [8192], P('dp'), may hold values 0 or 1
- sample_weight: float32 [8192], P('dp'), may hold values from 0.3 to 9
- weight_in: bfloat16 [1024, 8192], P(None, 'mp'), may hold values from -0.1875 to 0.1875
- bias_in: float32 [8192], P('mp'), may hold values from -3 to 3
- weight_out: bfloat16 [8192], P('mp'), may hold values from -0.0625 to 0.0625
- dense_accum: float32 [1024, 8192], P('dp', 'mp'), may hold values from 1e-08 to 1e-06
- table_rows: float32 [131072, 64], P(('dp', 'mp')), may hold values from -0.12 to 0.12
- table_accum: float32 [131072], P(('dp', 'mp')), may hold values from 1e-12 to 1e-05
Outputs:
- weight_new: bfloat16 [1024, 8192], P(None, 'mp')
- accum_new: float32 [1024, 8192], P('dp', 'mp')
- table_new: float32 [131072, 64], P(('dp', 'mp'))
- table_accum_new: float32 [131072], P(('dp', 'mp'))
Inputs may be any that keep to these rules, and one draw needn't show every extreme that they name: `row_ids`: the first peer_counts entries of each device's list for an owner are distinct rows of that owner's shard. `peer_counts`: some owner has 32 touched rows on every device, and some device has 32 touched rows of every owner. `lookup_slots`: below the sum of that device's peer_counts; every device has a lookup of its last touched row.
All inputs are finite; a program needn't handle non-finite values. No bound on the sum of `labels` on one device may be relied on, other than what follows from the above.
Results may differ from a plain program's by a relative error of at most 0.0034.
Values may be sent and summed in bfloat16 or wider, within the bound.
A program may use at most 128 MiB of HBM per device.

v0:
```python
import jax
import jax.numpy as jnp
from jax import lax
from jax.sharding import PartitionSpec as P

clip_norm = 1.0
dense_rate = 0.02
table_rate = 0.5
adagrad_eps = 1e-10


def slot_index(compact, counts, capacity):
    slot_ends = jnp.cumsum(counts)
    owner_index = jnp.sum((compact[..., None] >= slot_ends).astype(jnp.int32), axis=-1)
    slot_starts = slot_ends - counts
    owner_match = owner_index[..., None] == jnp.arange(counts.shape[0], dtype=jnp.int32)
    owner_begin = jnp.sum(jnp.where(owner_match, slot_starts, 0), axis=-1)
    return owner_index * capacity + compact - owner_begin


def body(
    slab_values,
    row_ids,
    peer_counts,
    lookup_slots,
    labels,
    sample_weight,
    weight_in,
    bias_in,
    weight_out,
    dense_accum,
    table_rows,
    table_accum,
):
    peers = peer_counts.shape[1]
    capacity = row_ids.shape[2]
    emb_width = slab_values.shape[2] // capacity
    batch = lookup_slots.shape[0]
    features = lookup_slots.shape[1]
    index = slot_index(lookup_slots, peer_counts[0], capacity)
    slab_view = slab_values[0].reshape(peers * capacity, emb_width)
    pooled = slab_view[index].reshape(batch, features * emb_width)
    group = lax.all_gather(pooled, "mp", axis=0, tiled=True)
    act = jnp.dot(group, weight_in, preferred_element_type=jnp.float32) + bias_in
    hidden = jax.nn.silu(act).astype(jnp.bfloat16)
    logit = lax.psum(jnp.dot(hidden, weight_out, preferred_element_type=jnp.float32), "mp")
    dlogit = sample_weight * (jax.nn.sigmoid(logit) - labels.astype(jnp.float32))
    sigma = jax.nn.sigmoid(act)
    dact = (
        dlogit[:, None]
        * weight_out.astype(jnp.float32)[None, :]
        * sigma
        * (1.0 + act * (1.0 - sigma))
    ).astype(jnp.bfloat16)
    dpooled = lax.psum_scatter(
        lax.dot_general(
            dact, weight_in, (((1,), (1,)), ((), ())), preferred_element_type=jnp.float32
        ),
        "mp",
        scatter_dimension=0,
        tiled=True,
    )
    slot_grad = jax.ops.segment_sum(
        dpooled.reshape(batch * features, emb_width),
        index.reshape(-1),
        num_segments=peers * capacity,
    )
    grad_in = lax.dot_general(
        group, dact, (((0,), (0,)), ((), ())), preferred_element_type=jnp.float32
    )
    grad_bias = jnp.sum(dact.astype(jnp.float32), axis=0)
    grad_out = jnp.dot(dlogit, hidden.astype(jnp.float32), precision=lax.Precision.HIGHEST)
    first_group = (lax.axis_index("dp") == 0).astype(jnp.float32)
    own_rows = dense_accum.shape[0]
    row_start = lax.axis_index("dp") * own_rows
    grad_rows = lax.psum_scatter(grad_in, "dp", scatter_dimension=0, tiled=True)
    grad_bias, grad_out = lax.psum((grad_bias, grad_out), "dp")
    dense_square = jnp.sum(grad_rows * grad_rows)
    dense_square = dense_square + first_group * (
        jnp.sum(grad_bias * grad_bias) + jnp.sum(grad_out * grad_out)
    )
    total = lax.psum(dense_square + jnp.sum(slot_grad * slot_grad), ("dp", "mp"))
    scale = clip_norm / jnp.maximum(jnp.sqrt(total), clip_norm)
    clipped = scale * grad_rows
    accum_new = dense_accum + clipped * clipped
    weight_part = lax.dynamic_slice_in_dim(weight_in, row_start, own_rows, 0).astype(jnp.float32)
    updated = (weight_part - dense_rate * clipped / (jnp.sqrt(accum_new) + adagrad_eps)).astype(
        jnp.bfloat16
    )
    weight_new = lax.all_gather(updated, "dp", axis=0, tiled=True)
    row_values = row_ids[0].astype(jnp.float32)
    outgoing = (scale * slot_grad).reshape(peers, capacity * emb_width)
    arrived, arrived_rows = (
        lax.all_to_all(outgoing, ("dp", "mp"), split_axis=0, concat_axis=0, tiled=True),
        lax.all_to_all(row_values, ("dp", "mp"), split_axis=0, concat_axis=0, tiled=True),
    )
    received = jax.ops.segment_sum(
        arrived.reshape(-1, emb_width),
        arrived_rows.reshape(-1).astype(jnp.int32),
        num_segments=table_rows.shape[0],
    )
    table_accum_new = table_accum + jnp.mean(received * received, axis=1)
    table_new = table_rows - table_rate * received / (
        jnp.sqrt(table_accum_new)[:, None] + adagrad_eps
    )
    return (weight_new, accum_new, table_new, table_accum_new)


def solution(mesh):
    placed = (
        P(("dp", "mp"), None, None),
        P(("dp", "mp"), None, None),
        P(("dp", "mp"), None),
        P(("dp", "mp"), None),
        P("dp"),
        P("dp"),
        P(None, "mp"),
        P("mp"),
        P("mp"),
        P("dp", "mp"),
        P(("dp", "mp"), None),
        P(("dp", "mp")),
    )
    return jax.shard_map(
        body,
        mesh=mesh,
        in_specs=placed,
        out_specs=(P(None, "mp"), P("dp", "mp"), P(("dp", "mp"), None), P(("dp", "mp"))),
        check_vma=False,
    )
```

profile of v0, /device:TPU:0, one launch (start us, length us, event | category | flops | bytes accessed | tf_op | source)
XLA Modules:
  0.0 362.3 jit_solution(8915836303579359678)
XLA Ops:
  7.2 0.0 all-gather.3.cloned.1.call-start
  7.2 0.7 copy.34
  7.9 0.1 reduce-window.8
  8.0 0.1 reduce
  8.1 0.7 bitcast_subtract_fusion
  8.8 0.9 convert_reduce_fusion.1
  9.7 0.2 select_reduce_fusion
  9.8 0.7 compare_select_fusion
  10.5 0.1 copy.35
  10.6 0.1 reshape.86
  10.8 1.2 reshape_squeeze.3
  11.9 0.0 copy-start.4
  12.0 0.0 copy-start.7
  12.0 12.1 %gather_fusion = bf16[4096,64]{1,0:T(8,128)(2,1)S(1)} fusion(bf16[1024,64]{1,0:T(8,128)(2,1)S(1)} %reshape_squeeze.3, s32[4096]{0:T(1024)S(1)} %broadcast_clamp_fusion), kind=kCustom, calls=%fused_computation | custom fusion | bytes 1064960 | tf_op jit(solution)/shard_map/gather | solution.py:42
  24.1 1.5 reshape.81
  25.6 0.0 all-gather.3.cloned.1.call-update
  25.6 0.0 reduce-scatter.5.cloned.1.call-start
  25.7 48.5 %all-gather.3.cloned.1.call-done = bf16[1024,1024]{1,0:T(8,128)(2,1)} async-done(((bf16[256,1024]{1,0:T(8,128)(2,1)}), bf16[1024,1024]{1,0:T(8,128)(2,1)}) %all-gather.3.cloned.1.call-update) | async-done | bytes 2097168 | tf_op jit(solution)/shard_map/all_gather | solution.py:43
  74.2 11.2 %multiply_convert_fusion.1 = (bf16[1024,2048]{1,0:T(8,128)(2,1)S(1)}, f32[1024,2048]{1,0:T(8,128)}) fusion(f32[2048]{0:T(1024)S(1)} %copy-done.7, bf16[1024,1024]{1,0:T(8,128)(2,1)} %all-gather.3.cloned.1.call-done, bf16[1024,2048]{1,0:T(8,128)(2,1)} %param.18), kind=kOutput, calls=%fused_computation.5 | convolution fusion | flops 4307550208 | bytes 18882560 | tf_op jit(solution)/shard_map/dot_general | solution.py:44
  85.3 2.0 copy-done
  87.3 1.2 fusion.4
  88.5 9.7 %psum.28 = f32[1024]{0:T(1024)S(1)} all-reduce(f32[1024]{0:T(1024)S(1)} %bitcast.19), channel_id=1, replica_groups=mesh['dp'=8,'mp'=4] {'mp'}, use_global_device_ids=true, to_apply=%region_3.4 | all-reduce | flops 1024 | bytes 8192 | tf_op jit(solution)/shard_map/psum | solution.py:46
  98.2 0.0 copy-start.3
  98.2 6.1 %convert_reduce_fusion = (f32[2048]{0:T(1024)S(1)}, bf16[1024,2048]{1,0:T(8,128)(2,1)S(1)}) fusion(f32[1024,2048]{1,0:T(8,128)} %get-tuple-element.27, f32[2048]{0:T(1024)S(1)} %copy-done.7, f32[2048]{0:T(1024)S(1)} %convert_element_type.56, f32[1024]{0:T(1024)S(1)} %subtract_multiply_fusion), kind=kLoop, calls=%fused_computation.3 | loop fusion | flops 27260928 | bytes 12611584 | tf_op jit(solution)/shard_map/reduce_sum | solution.py:71
  104.4 0.0 copy-start.1
  104.4 2.0 copy-done.1
  106.4 6.1 %fusion.7 = f32[1024,1024]{1,0:T(8,128)} fusion(bf16[1024,2048]{1,0:T(8,128)(2,1)S(1)} %get-tuple-element.23, bf16[1024,2048]{1,0:T(8,128)(2,1)S(1)} %copy-done.3), kind=kOutput, calls=%fused_computation.34 | convolution fusion | flops 4294967296 | bytes 12582912 | tf_op jit(solution)/shard_map/dot_general | solution.py:56
  112.5 0.0 reduce-scatter.5.cloned.1.call-update
  112.5 0.2 reduce-scatter.3.cloned.1.call-start
  112.7 1.3 copy-done.10
  114.1 9.0 %fusion.5 = f32[1024,2048]{1,0:T(8,128)} fusion(bf16[1024,1024]{1,0:T(8,128)(2,1)S(1)} %copy-done.10, bf16[1024,2048]{1,0:T(8,128)(2,1)} %copy-done.1), kind=kOutput, calls=%fused_computation.32 | convolution fusion | flops 4294967296 | bytes 14680064 | tf_op jit(solution)/shard_map/dot_general | solution.py:68
  123.0 0.0 reduce-scatter.3.cloned.1.call-update
  123.0 0.0 all-gather.5.cloned.1.call-start
  123.1 0.1 copy.36
  123.2 0.1 reshape.94
  123.3 3.9 %fusion.6 = f32[1,2048]{1,0:T(1,128)S(1)} fusion(f32[1024,1]{0,1:T(1,128)S(1)} %bitcast.17, bf16[1024,2048]{1,0:T(8,128)(2,1)} %copy-done), kind=kOutput, calls=%fused_computation.33 | convolution fusion | flops 25165824 | bytes 4206592 | tf_op jit(solution)/shard_map/dot_general | solution.py:72
  127.2 22.8 %all-reduce = (f32[2048]{0:T(1024)S(1)}, f32[2048]{0:T(1024)S(1)}) all-reduce(f32[2048]{0:T(1024)S(1)} %get-tuple-element.22, f32[2048]{0:T(1024)S(1)} %bitcast.18), channel_id=1, replica_groups=mesh['dp'=8,'mp'=4] {'dp'}, use_global_device_ids=true, to_apply=%region_7.8 | all-reduce | flops 4096 | bytes 32768 | tf_op jit(solution)/shard_map/psum | solution.py:77
  150.0 0.6 multiply_reduce_fusion.3
  151.9 35.8 %reduce-scatter.5.cloned.1.call-done = f32[256,1024]{1,0:T(8,128)} async-done(((f32[1024,1024]{1,0:T(8,128)}), f32[256,1024]{1,0:T(8,128)}) %reduce-scatter.5.cloned.1.call-update) | async-done | bytes 1048592 | tf_op jit(solution)/shard_map/reduce_scatter | solution.py:55
  187.7 1.7 reshape.96
  189.4 22.5 %scatter_custom_fusion = f32[1024,64]{1,0:T(8,128)S(1)} fusion(s32[4096]{0:T(1024)S(1)} %reshape.94, f32[4096,64]{1,0:T(8,128)S(1)} %reshape.96, f32[]{:T(128)} %constant.19.clone.1), kind=kCustom, calls=%fused_computation.19 | custom fusion | flops 262144 | bytes 262148 | tf_op jit(solution)/shard_map/scatter-add | solution.py:63
  211.9 0.7 multiply_reduce_fusion.2
  212.6 50.6 %reduce-scatter.3.cloned.1.call-done = f32[128,2048]{1,0:T(8,128)} async-done(((f32[1024,2048]{1,0:T(8,128)}), f32[128,2048]{1,0:T(8,128)}) %reduce-scatter.3.cloned.1.call-update) | async-done | bytes 1048592 | tf_op jit(solution)/shard_map/reduce_scatter | solution.py:76
  263.2 2.1 multiply_reduce_fusion.1
  266.6 39.3 %psum.31 = f32[]{:T(128)} all-reduce(f32[]{:T(128)S(6)} %add.86), channel_id=1, replica_groups=mesh['dp'=8,'mp'=4] {'dp','mp'}, use_global_device_ids=true, to_apply=%region_14.15 | all-reduce | flops 1 | bytes 8 | tf_op jit(solution)/shard_map/psum | solution.py:82
  306.6 3.4 subtract_convert_fusion
  310.0 0.0 all-gather.5.cloned.1.call-update
  310.1 0.6 convert_element_type.60
  310.7 5.6 %all-to-all-start = ((f32[32,1,32]{2,1,0:T(1,128)}), f32[32,1,32]{2,1,0:T(1,128)S(1)}, u32[]{:S(2)}, u32[]{:S(2)}) async-start(f32[32,1,32]{2,1,0:T(1,128)} %bitcast.5), calls=%async_computation.2 | async-start | bytes 32768 | tf_op jit(solution)/shard_map/all_to_all | solution.py:95
  316.3 1.0 all_to_all.13
  317.3 6.1 %all-to-all-done = f32[32,1,32]{2,1,0:T(1,128)S(1)} async-done(((f32[32,1,32]{2,1,0:T(1,128)}), f32[32,1,32]{2,1,0:T(1,128)S(1)}, u32[]{:S(2)}, u32[]{:S(2)}) %all-to-all-start) | async-done | bytes 4128 | tf_op jit(solution)/shard_map/all_to_all | solution.py:95
  323.4 2.8 all-to-all-start.1
  326.2 1.9 copy.38
  328.1 0.1 convert_reduce_fusion.2
  328.2 0.1 reshape.102
  328.3 8.0 %all-to-all-done.1 = f32[32,1,2048]{2,1,0:T(1,128)S(1)} async-done(((f32[32,1,2048]{2,1,0:T(1,128)}), f32[32,1,2048]{2,1,0:T(1,128)S(1)}, u32[]{:S(2)}, u32[]{:S(2)}) %all-to-all-start.1) | async-done | bytes 262176 | tf_op jit(solution)/shard_map/all_to_all | solution.py:94
  336.3 0.6 reduce.2
  336.9 0.2 reshape.104
  337.1 6.5 %scatter_custom_fusion.1 = f32[4096,64]{1,0:T(8,128)S(1)} fusion(s32[1024]{0:T(1024)S(1)} %reshape.102, f32[1024,64]{1,0:T(8,128)S(1)} %reshape.104, f32[]{:T(128)} %constant.19.clone.1), kind=kCustom, calls=%fused_computation.9 | custom fusion | flops 65536 | bytes 1048580 | tf_op jit(solution)/shard_map/scatter-add | solution.py:97
  343.7 0.6 multiply_reduce_fusion
  344.3 0.6 sqrt_add_fusion
  344.9 2.9 divide_subtract_fusion
  347.8 3.1 copy.39
  350.9 4.8 %copy.41 = bf16[1024,2048]{1,0:T(8,128)(2,1)} copy(bf16[1024,2048]{1,0:T(8,128)(2,1)} %all-gather.5.cloned.1.call-done) | data formatting | bytes 8388608
  (21 shorter events, 0.1 us)
Async XLA Ops:
  7.2 67.0 %all-gather.3.cloned.1.call-start = ((), (), s32[]{:S(2)}) async-start(), calls=%async_computation.4 | async-start | bytes 2621440 | tf_op jit(solution)/shard_map/all_gather | solution.py:43
  11.9 13.8 %copy-start.4 = (bf16[2048]{0:T(1024)(128)(2,1)S(1)}, bf16[2048]{0:T(1024)(128)(2,1)}, u32[]{:S(2)}) copy-start(bf16[2048]{0:T(1024)(128)(2,1)} %param.20) | copy-start | bytes 12292
  12.0 62.2 %copy-start.7 = (f32[2048]{0:T(1024)S(1)}, f32[2048]{0:T(1024)}, u32[]{:S(2)}) copy-start(f32[2048]{0:T(1024)} %param.19) | copy-start | bytes 24580
  25.6 162.0 %reduce-scatter.5.cloned.1.call-start = ((), (), s32[]{:S(2)}) async-start(), calls=%async_computation.6 | async-start | bytes 5242880 | tf_op jit(solution)/shard_map/reduce_scatter | solution.py:55
  85.3 2.0 copy-start
  85.3 12.9 %copy-start.8 = (f32[1024]{0:T(1024)S(1)}, f32[1024]{0:T(1024)}, u32[]{:S(2)}) copy-start(f32[1024]{0:T(1024)} %param.17) | copy-start | bytes 12292
  85.3 12.9 %copy-start.9 = (s32[1024]{0:T(1024)S(1)}, s32[1024]{0:T(1024)}, u32[]{:S(2)}) copy-start(s32[1024]{0:T(1024)} %param.16) | copy-start | bytes 12292
  98.2 8.1 %copy-start.3 = (bf16[1024,2048]{1,0:T(8,128)(2,1)S(1)}, bf16[1024,2048]{1,0:T(8,128)(2,1)}, u32[]{:S(2)}) copy-start(bf16[1024,2048]{1,0:T(8,128)(2,1)} %param.18) | copy-start | bytes 12582916
  104.4 2.0 copy-start.1
  112.5 1.6 copy-start.10
  112.5 150.7 %reduce-scatter.3.cloned.1.call-start = ((), (), s32[]{:S(2)}) async-start(), calls=%async_computation.5 | async-start | bytes 9437184 | tf_op jit(solution)/shard_map/reduce_scatter | solution.py:76
  123.0 227.9 %all-gather.5.cloned.1.call-start = ((), (), s32[]{:S(2)}) async-start(), calls=%async_computation.7 | async-start | bytes 4718592 | tf_op jit(solution)/shard_map/all_gather | solution.py:90
  189.4 120.7 %copy-start.5 = (s32[1,32,32]{2,1,0:T(8,128)S(1)}, s32[1,32,32]{2,1,0:T(8,128)}, u32[]{:S(2)}) copy-start(s32[1,32,32]{2,1,0:T(8,128)} %param.13) | copy-start | bytes 12292
  212.6 113.6 %copy-start.2 = (f32[4096,64]{0,1:T(8,128)S(1)}, f32[4096,64]{0,1:T(8,128)}, u32[]{:S(2)}) copy-start(f32[4096,64]{0,1:T(8,128)} %param.22) | copy-start | bytes 3145732
  310.7 12.7 %all-to-all-start = ((f32[32,1,32]{2,1,0:T(1,128)}), f32[32,1,32]{2,1,0:T(1,128)S(1)}, u32[]{:S(2)}, u32[]{:S(2)}) async-start(f32[32,1,32]{2,1,0:T(1,128)} %bitcast.5), calls=%async_computation.2 | async-start | bytes 32768 | tf_op jit(solution)/shard_map/all_to_all | solution.py:95
  323.4 12.9 %all-to-all-start.1 = ((f32[32,1,2048]{2,1,0:T(1,128)}), f32[32,1,2048]{2,1,0:T(1,128)S(1)}, u32[]{:S(2)}, u32[]{:S(2)}) async-start(f32[32,1,2048]{2,1,0:T(1,128)} %all_to_all.13), calls=%async_computation.3 | async-start | bytes 524288 | tf_op jit(solution)/shard_map/all_to_all | solution.py:94
  326.2 18.1 %copy-start.6 = (f32[4096]{0:T(1024)S(1)}, f32[4096]{0:T(1024)}, u32[]{:S(2)}) copy-start(f32[4096]{0:T(1024)} %param.23) | copy-start | bytes 49156
Sparse Core Ops, SparseCore 0:
  25.8 48.3 all-gather.2
  112.6 74.9 reduce-scatter.4
  191.1 72.0 reduce-scatter.2
  310.2 37.9 all-gather.4
where the time goes:
time: 363 us; the launch traced here: 362 us
  waiting for transfers between devices  149 us (41%)
  blocking collectives  71.8 us (20%)
  other arithmetic  50 us (14%)
  local copies, waits for them, and re-layouts  34.2 us (9%)
  matrix products  31.3 us (9%)
  between operations  17.4 us (5%)
  starting transfers between devices  8.71 us (2%)
    reduce_scatter x1, waiting for transfers between devices, body(): grad_rows = lax.psum_scatter(grad_in, 'dp', scatter_dimension=0, tiled=True)  50.6 us
    all_gather x1, waiting for transfers between devices, body(): group = lax.all_gather(pooled, 'mp', axis=0, tiled=True)  48.5 us
    psum x1, blocking collectives, body(): lax.psum(dense_square + jnp.sum(slot_grad * slot_grad), ('dp', 'mp'))  39.3 us
    reduce_scatter x1, waiting for transfers between devices, body(): lax.psum_scatter(lax.dot_general(dact, weight_in, (((1,), (1,)), ((), ())...  35.8 us
    psum x1, blocking collectives, body(): grad_bias, grad_out = lax.psum((grad_bias, grad_out), 'dp')  22.8 us
    scatter-add x1, other arithmetic, body(): jax.ops.segment_sum(dpooled.reshape(batch * features, emb_width), index.r...  22.5 us
    unnamed x26, local copies, waits for them, and re-layouts  15.2 us
    gather x1, local copies, waits for them, and re-layouts, body(): pooled = slab_view[index].reshape(batch, features * emb_width)  12.1 us
  transfers between devices with their start and end apart: 6, of which 5 were waited for; matrix products, arithmetic and copies ran while one was open for 15% of the time, Pallas kernels for 0%

commit v1 on v0

--- a/solution.py
+++ b/solution.py
@@ -79,7 +79,9 @@
     dense_square = dense_square + first_group * (
         jnp.sum(grad_bias * grad_bias) + jnp.sum(grad_out * grad_out)
     )
-    total = lax.psum(dense_square + jnp.sum(slot_grad * slot_grad), ("dp", "mp"))
+    total = jnp.sum(
+        lax.all_gather(dense_square + jnp.sum(slot_grad * slot_grad), ("dp", "mp")), axis=0
+    )
     scale = clip_norm / jnp.maximum(jnp.sqrt(total), clip_norm)
     clipped = scale * grad_rows
     accum_new = dense_accum + clipped * clipped

time: 363 us -> 364 us (level)
    psum x1 -> x0, blocking collectives: 39.3 us -> none  [body(): lax.psum(dense_square + jnp.sum(slot_grad * slot_grad), ('dp', 'mp'))]
    unnamed x0 -> x1, blocking collectives: none -> 39.2 us
    unnamed x26 -> x28, local copies, waits for them, and re-layouts: 15.2 us -> 15.3 us
where the time goes in v1:
time: 364 us; the launch traced here: 363 us
  waiting for transfers between devices  149 us (41%)
  blocking collectives  71.7 us (20%)
  other arithmetic  50.6 us (14%)
  local copies, waits for them, and re-layouts  34.3 us (9%)
  matrix products  31.3 us (9%)
  between operations  17.4 us (5%)
  starting transfers between devices  8.52 us (2%)
    reduce_scatter x1, waiting for transfers between devices, body(): grad_rows = lax.psum_scatter(grad_in, 'dp', scatter_dimension=0, tiled=True)  50.6 us
    all_gather x1, waiting for transfers between devices, body(): group = lax.all_gather(pooled, 'mp', axis=0, tiled=True)  48.5 us
    unnamed x1, blocking collectives  39.2 us
    reduce_scatter x1, waiting for transfers between devices, body(): lax.psum_scatter(lax.dot_general(dact, weight_in, (((1,), (1,)), ((), ())...  35.8 us
    psum x1, blocking collectives, body(): grad_bias, grad_out = lax.psum((grad_bias, grad_out), 'dp')  22.8 us
    scatter-add x1, other arithmetic, body(): jax.ops.segment_sum(dpooled.reshape(batch * features, emb_width), index.r...  22.5 us
    unnamed x28, local copies, waits for them, and re-layouts  15.3 us
    gather x1, local copies, waits for them, and re-layouts, body(): pooled = slab_view[index].reshape(batch, features * emb_width)  12.1 us
  transfers between devices with their start and end apart: 6, of which 5 were waited for; matrix products, arithmetic and copies ran while one was open for 15% of the time, Pallas kernels for 0%

profile of v1, /device:TPU:0, one launch (start us, length us, event | category | flops | bytes accessed | tf_op | source)
XLA Modules:
  0.0 362.8 jit_solution(1748825777367017277)
XLA Ops:
  7.2 0.0 all-gather.3.cloned.1.call-start
  7.2 0.7 copy.34
  7.9 0.1 reduce-window.8
  8.0 0.1 reduce.1
  8.1 0.7 bitcast_subtract_fusion
  8.8 0.9 convert_reduce_fusion.1
  9.7 0.2 select_reduce_fusion
  9.8 0.7 compare_select_fusion
  10.5 0.1 copy.35
  10.6 0.1 reshape.86
  10.8 1.2 reshape_squeeze.3
  11.9 0.0 copy-start.4
  12.0 0.0 copy-start.7
  12.0 12.1 %gather_fusion = bf16[4096,64]{1,0:T(8,128)(2,1)S(1)} fusion(bf16[1024,64]{1,0:T(8,128)(2,1)S(1)} %reshape_squeeze.3, s32[4096]{0:T(1024)S(1)} %broadcast_clamp_fusion), kind=kCustom, calls=%fused_computation | custom fusion | bytes 1064960 | tf_op jit(solution)/shard_map/gather | solution.py:42
  24.1 1.5 reshape.81
  25.6 0.0 all-gather.3.cloned.1.call-update
  25.6 0.0 reduce-scatter.5.cloned.1.call-start
  25.7 48.5 %all-gather.3.cloned.1.call-done = bf16[1024,1024]{1,0:T(8,128)(2,1)} async-done(((bf16[256,1024]{1,0:T(8,128)(2,1)}), bf16[1024,1024]{1,0:T(8,128)(2,1)}) %all-gather.3.cloned.1.call-update) | async-done | bytes 2097168 | tf_op jit(solution)/shard_map/all_gather | solution.py:43
  74.2 11.2 %multiply_convert_fusion.1 = (bf16[1024,2048]{1,0:T(8,128)(2,1)S(1)}, f32[1024,2048]{1,0:T(8,128)}) fusion(f32[2048]{0:T(1024)S(1)} %copy-done.7, bf16[1024,1024]{1,0:T(8,128)(2,1)} %all-gather.3.cloned.1.call-done, bf16[1024,2048]{1,0:T(8,128)(2,1)} %param.18), kind=kOutput, calls=%fused_computation.5 | convolution fusion | flops 4307550208 | bytes 18882560 | tf_op jit(solution)/shard_map/dot_general | solution.py:44
  85.3 2.0 copy-done
  87.3 1.2 fusion.4
  88.5 9.7 %psum.21 = f32[1024]{0:T(1024)S(1)} all-reduce(f32[1024]{0:T(1024)S(1)} %bitcast.20), channel_id=1, replica_groups=mesh['dp'=8,'mp'=4] {'mp'}, use_global_device_ids=true, to_apply=%region_3.4 | all-reduce | flops 1024 | bytes 8192 | tf_op jit(solution)/shard_map/psum | solution.py:46
  98.2 6.1 %convert_reduce_fusion = (f32[2048]{0:T(1024)S(1)}, bf16[1024,2048]{1,0:T(8,128)(2,1)S(1)}) fusion(f32[1024,2048]{1,0:T(8,128)} %get-tuple-element.27, f32[2048]{0:T(1024)S(1)} %copy-done.7, f32[2048]{0:T(1024)S(1)} %convert_element_type.56, f32[1024]{0:T(1024)S(1)} %subtract_multiply_fusion), kind=kLoop, calls=%fused_computation.3 | loop fusion | flops 27260928 | bytes 12611584 | tf_op jit(solution)/shard_map/reduce_sum | solution.py:71
  104.4 2.0 copy-done.1
  106.4 6.1 %fusion.7 = f32[1024,1024]{1,0:T(8,128)} fusion(bf16[1024,2048]{1,0:T(8,128)(2,1)S(1)} %get-tuple-element.23, bf16[1024,2048]{1,0:T(8,128)(2,1)S(1)} %copy-done.3), kind=kOutput, calls=%fused_computation.34 | convolution fusion | flops 4294967296 | bytes 12582912 | tf_op jit(solution)/shard_map/dot_general | solution.py:56
  112.5 0.0 reduce-scatter.5.cloned.1.call-update
  112.5 0.2 reduce-scatter.3.cloned.1.call-start
  112.7 1.3 copy-done.10
  114.1 9.0 %fusion.5 = f32[1024,2048]{1,0:T(8,128)} fusion(bf16[1024,1024]{1,0:T(8,128)(2,1)S(1)} %copy-done.10, bf16[1024,2048]{1,0:T(8,128)(2,1)} %copy-done.1), kind=kOutput, calls=%fused_computation.32 | convolution fusion | flops 4294967296 | bytes 14680064 | tf_op jit(solution)/shard_map/dot_general | solution.py:68
  123.0 0.0 reduce-scatter.3.cloned.1.call-update
  123.0 0.0 all-gather.5.cloned.1.call-start
  123.1 0.1 copy.36
  123.2 0.1 reshape.94
  123.3 3.9 %fusion.6 = f32[1,2048]{1,0:T(1,128)S(1)} fusion(f32[1024,1]{0,1:T(1,128)S(1)} %bitcast.18, bf16[1024,2048]{1,0:T(8,128)(2,1)} %copy-done), kind=kOutput, calls=%fused_computation.33 | convolution fusion | flops 25165824 | bytes 4206592 | tf_op jit(solution)/shard_map/dot_general | solution.py:72
  127.2 22.8 %all-reduce.1 = (f32[2048]{0:T(1024)S(1)}, f32[2048]{0:T(1024)S(1)}) all-reduce(f32[2048]{0:T(1024)S(1)} %get-tuple-element.22, f32[2048]{0:T(1024)S(1)} %bitcast.19), channel_id=1, replica_groups=mesh['dp'=8,'mp'=4] {'dp'}, use_global_device_ids=true, to_apply=%region_7.8 | all-reduce | flops 4096 | bytes 32768 | tf_op jit(solution)/shard_map/psum | solution.py:77
  150.0 0.6 multiply_reduce_fusion.3
  151.9 35.8 %reduce-scatter.5.cloned.1.call-done = f32[256,1024]{1,0:T(8,128)} async-done(((f32[1024,1024]{1,0:T(8,128)}), f32[256,1024]{1,0:T(8,128)}) %reduce-scatter.5.cloned.1.call-update) | async-done | bytes 1048592 | tf_op jit(solution)/shard_map/reduce_scatter | solution.py:55
  187.7 1.7 reshape.96
  189.4 22.5 %scatter_custom_fusion = f32[1024,64]{1,0:T(8,128)S(1)} fusion(s32[4096]{0:T(1024)S(1)} %reshape.94, f32[4096,64]{1,0:T(8,128)S(1)} %reshape.96, f32[]{:T(128)} %constant.19.clone.1), kind=kCustom, calls=%fused_computation.19 | custom fusion | flops 262144 | bytes 262148 | tf_op jit(solution)/shard_map/scatter-add | solution.py:63
  211.9 0.7 multiply_reduce_fusion.2
  212.6 50.6 %reduce-scatter.3.cloned.1.call-done = f32[128,2048]{1,0:T(8,128)} async-done(((f32[1024,2048]{1,0:T(8,128)}), f32[128,2048]{1,0:T(8,128)}) %reduce-scatter.3.cloned.1.call-update) | async-done | bytes 1048592 | tf_op jit(solution)/shard_map/reduce_scatter | solution.py:76
  263.2 2.1 multiply_reduce_fusion.1
  266.6 0.1 dynamic-update-slice
  266.7 39.2 %all-reduce = f32[32]{0:T(128)S(1)} all-reduce(f32[32]{0:T(128)S(1)} %dynamic-update-slice), channel_id=1, replica_groups=mesh['dp'=8,'mp'=4] {'dp','mp'}, use_global_device_ids=true, to_apply=%add | all-reduce | flops 32 | bytes 256
  305.9 0.6 reduce_sum.88
  307.3 3.4 subtract_convert_fusion
  310.7 0.0 all-gather.5.cloned.1.call-update
  310.7 0.6 convert_element_type.60
  311.3 5.4 %all-to-all-start = ((f32[32,1,32]{2,1,0:T(1,128)}), f32[32,1,32]{2,1,0:T(1,128)S(1)}, u32[]{:S(2)}, u32[]{:S(2)}) async-start(f32[32,1,32]{2,1,0:T(1,128)} %bitcast.6), calls=%async_computation.2 | async-start | bytes 32768 | tf_op jit(solution)/shard_map/all_to_all | solution.py:97
  316.8 1.0 all_to_all.13
  317.8 6.1 %all-to-all-done = f32[32,1,32]{2,1,0:T(1,128)S(1)} async-done(((f32[32,1,32]{2,1,0:T(1,128)}), f32[32,1,32]{2,1,0:T(1,128)S(1)}, u32[]{:S(2)}, u32[]{:S(2)}) %all-to-all-start) | async-done | bytes 4128 | tf_op jit(solution)/shard_map/all_to_all | solution.py:97
  323.8 2.8 all-to-all-start.1
  326.7 1.9 copy.38
  328.6 0.1 convert_reduce_fusion.2
  328.7 0.1 reshape.102
  328.7 8.0 %all-to-all-done.1 = f32[32,1,2048]{2,1,0:T(1,128)S(1)} async-done(((f32[32,1,2048]{2,1,0:T(1,128)}), f32[32,1,2048]{2,1,0:T(1,128)S(1)}, u32[]{:S(2)}, u32[]{:S(2)}) %all-to-all-start.1) | async-done | bytes 262176 | tf_op jit(solution)/shard_map/all_to_all | solution.py:96
  336.8 0.6 reduce.3
  337.4 0.2 reshape.104
  337.6 6.5 %scatter_custom_fusion.1 = f32[4096,64]{1,0:T(8,128)S(1)} fusion(s32[1024]{0:T(1024)S(1)} %reshape.102, f32[1024,64]{1,0:T(8,128)S(1)} %reshape.104, f32[]{:T(128)} %constant.19.clone.1), kind=kCustom, calls=%fused_computation.9 | custom fusion | flops 65536 | bytes 1048580 | tf_op jit(solution)/shard_map/scatter-add | solution.py:99
  344.1 0.6 multiply_reduce_fusion
  344.8 0.6 sqrt_add_fusion
  345.4 2.9 divide_subtract_fusion
  348.3 3.1 copy.39
  351.4 4.8 %copy.42 = bf16[1024,2048]{1,0:T(8,128)(2,1)} copy(bf16[1024,2048]{1,0:T(8,128)(2,1)} %all-gather.5.cloned.1.call-done) | data formatting | bytes 8388608
  (24 shorter events, 0.1 us)
Async XLA Ops:
  7.2 67.0 %all-gather.3.cloned.1.call-start = ((), (), s32[]{:S(2)}) async-start(), calls=%async_computation.4 | async-start | bytes 2621440 | tf_op jit(solution)/shard_map/all_gather | solution.py:43
  11.9 13.8 %copy-start.4 = (bf16[2048]{0:T(1024)(128)(2,1)S(1)}, bf16[2048]{0:T(1024)(128)(2,1)}, u32[]{:S(2)}) copy-start(bf16[2048]{0:T(1024)(128)(2,1)} %param.20) | copy-start | bytes 12292
  12.0 62.2 %copy-start.7 = (f32[2048]{0:T(1024)S(1)}, f32[2048]{0:T(1024)}, u32[]{:S(2)}) copy-start(f32[2048]{0:T(1024)} %param.19) | copy-start | bytes 24580
  25.6 162.0 %reduce-scatter.5.cloned.1.call-start = ((), (), s32[]{:S(2)}) async-start(), calls=%async_computation.6 | async-start | bytes 5242880 | tf_op jit(solution)/shard_map/reduce_scatter | solution.py:55
  85.3 2.0 copy-start
  85.3 12.9 %copy-start.8 = (f32[1024]{0:T(1024)S(1)}, f32[1024]{0:T(1024)}, u32[]{:S(2)}) copy-start(f32[1024]{0:T(1024)} %param.17) | copy-start | bytes 12292
  85.3 12.9 %copy-start.9 = (s32[1024]{0:T(1024)S(1)}, s32[1024]{0:T(1024)}, u32[]{:S(2)}) copy-start(s32[1024]{0:T(1024)} %param.16) | copy-start | bytes 12292
  98.2 8.1 %copy-start.3 = (bf16[1024,2048]{1,0:T(8,128)(2,1)S(1)}, bf16[1024,2048]{1,0:T(8,128)(2,1)}, u32[]{:S(2)}) copy-start(bf16[1024,2048]{1,0:T(8,128)(2,1)} %param.18) | copy-start | bytes 12582916
  104.4 2.0 copy-start.1
  112.5 1.6 copy-start.10
  112.5 150.7 %reduce-scatter.3.cloned.1.call-start = ((), (), s32[]{:S(2)}) async-start(), calls=%async_computation.5 | async-start | bytes 9437184 | tf_op jit(solution)/shard_map/reduce_scatter | solution.py:76
  123.0 228.4 %all-gather.5.cloned.1.call-start = ((), (), s32[]{:S(2)}) async-start(), calls=%async_computation.7 | async-start | bytes 4718592 | tf_op jit(solution)/shard_map/all_gather | solution.py:92
  189.4 121.4 %copy-start.5 = (s32[1,32,32]{2,1,0:T(8,128)S(1)}, s32[1,32,32]{2,1,0:T(8,128)}, u32[]{:S(2)}) copy-start(s32[1,32,32]{2,1,0:T(8,128)} %param.13) | copy-start | bytes 12292
  212.6 114.1 %copy-start.2 = (f32[4096,64]{0,1:T(8,128)S(1)}, f32[4096,64]{0,1:T(8,128)}, u32[]{:S(2)}) copy-start(f32[4096,64]{0,1:T(8,128)} %param.22) | copy-start | bytes 3145732
  311.3 12.5 %all-to-all-start = ((f32[32,1,32]{2,1,0:T(1,128)}), f32[32,1,32]{2,1,0:T(1,128)S(1)}, u32[]{:S(2)}, u32[]{:S(2)}) async-start(f32[32,1,32]{2,1,0:T(1,128)} %bitcast.6), calls=%async_computation.2 | async-start | bytes 32768 | tf_op jit(solution)/shard_map/all_to_all | solution.py:97
  323.8 12.9 %all-to-all-start.1 = ((f32[32,1,2048]{2,1,0:T(1,128)}), f32[32,1,2048]{2,1,0:T(1,128)S(1)}, u32[]{:S(2)}, u32[]{:S(2)}) async-start(f32[32,1,2048]{2,1,0:T(1,128)} %all_to_all.13), calls=%async_computation.3 | async-start | bytes 524288 | tf_op jit(solution)/shard_map/all_to_all | solution.py:96
  326.7 18.1 %copy-start.6 = (f32[4096]{0:T(1024)S(1)}, f32[4096]{0:T(1024)}, u32[]{:S(2)}) copy-start(f32[4096]{0:T(1024)} %param.23) | copy-start | bytes 49156
Sparse Core Ops, SparseCore 0:
  25.8 48.3 all-gather.2
  112.6 74.9 reduce-scatter.4
  191.1 72.0 reduce-scatter.2
  310.8 37.7 all-gather.4
